TPU v7x, 32 devices: a whole 2x2x4 slice. The times are simulated.
32 devices in a mesh: dp: 8 (over y, x, core), expert: 4 (over z).
Axes of the slice: x: 2, y: 2, z: 4, core: 2. Of those that a mesh axis runs over, the one named last changes fastest.
Arguments:
- policy_hidden: bfloat16 [1024, 4096], P('dp', 'expert'), may hold values from -6 to 6
- reference_hidden: bfloat16 [1024, 4096], P('dp', 'expert'), may hold values from -6 to 6
- policy_norm_gain: float32 [4096], P('expert'), may hold values from 0.25 to 1.75
- reference_norm_gain: float32 [4096], P('expert'), may hold values from 0.25 to 1.75
- policy_router: float32 [4096, 4], P('expert'), may hold values from -5.1875 to 5.1875
- reference_router: float32 [4096, 4], P('expert'), may hold values from -5.1875 to 5.1875
- policy_gate: bfloat16 [4, 4096, 8192], P('expert', 'dp'), may hold values from -0.09375 to 0.09375
- policy_up: bfloat16 [4, 4096, 8192], P('expert', 'dp'), may hold values from -0.09375 to 0.09375
- policy_down: bfloat16 [4, 8192, 4096], P('expert', 'dp'), may hold values from -0.0625 to 0.0625
- reference_gate: bfloat16 [4, 4096, 8192], P('expert', 'dp'), may hold values from -0.09375 to 0.09375
- reference_up: bfloat16 [4, 4096, 8192], P('expert', 'dp'), may hold values from -0.09375 to 0.09375
- reference_down: bfloat16 [4, 8192, 4096], P('expert', 'dp'), may hold values from -0.0625 to 0.0625
- expert_ids: int32 [1024, 2], P('dp'), may hold values from 0 to 3, all different within a row; in each aligned block of 128 rows (0 to 127, 128 to 255, ...) at most 96 rows name the same one
- lengths: int32 [32], P('dp'), may hold values from 1 to 32, as said below
Outputs:
- policy_mixture: bfloat16 [1024, 4096], P('dp', 'expert')
- reference_mixture: bfloat16 [1024, 4096], P('dp', 'expert')
- token_kl: float32 [1024], P('dp')
- loss: float32 [], replicated
Inputs may be any that keep to these rules, and one draw needn't show every extreme that they name: `expert_ids`: each row names 2 different experts; among the rows of one index of dp (aligned blocks of 128 rows) no expert is named more than 96 times, and in some block one expert is named exactly 96 times. The first lengths[r] of rollout r's 32 positions are live.
All inputs are finite; a program needn't handle non-finite values.
Results may differ from a plain program's by a relative error of at most 0.02.
Values may be sent and summed in bfloat16 or wider, within the bound.
A program may use at most 256 MiB of HBM per device.

v0:
```python
import jax
import jax.numpy as jnp
from jax import lax
from jax.sharding import PartitionSpec as P

D = 4096
SEG = 32
EPSILON = 1e-05
KL_WEIGHT = 1.0
BALANCE_WEIGHT = 0.5


def router_terms(hidden, norm_gain, router):
    values = hidden.astype(jnp.float32)
    partial_logits = jnp.dot(values * norm_gain, router, precision=lax.Precision.HIGHEST)
    return (partial_logits, jnp.sum(values * values, axis=1))


def expert_terms(piece_rows, weights):
    results = []
    for model_index in range(len(weights)):
        gate_weight, up_weight, down_weight = weights[model_index]
        model_rows = piece_rows[:, model_index, :]
        gate_value = jnp.dot(model_rows, gate_weight, preferred_element_type=jnp.float32)
        up_value = jnp.dot(model_rows, up_weight, preferred_element_type=jnp.float32)
        hidden = (jax.nn.silu(gate_value) * up_value).astype(jnp.bfloat16)
        results.append(jnp.dot(hidden, down_weight, preferred_element_type=jnp.float32))
    return jnp.stack(results, axis=1)


def mixture(slot_rows, weights):
    expert_count, slot_count, models, feature_block = slot_rows.shape
    model_width = expert_count * feature_block
    arrived_rows = lax.all_to_all(slot_rows, "expert", split_axis=0, concat_axis=3, tiled=True)
    local_rows = arrived_rows.reshape(slot_count, models, model_width)
    partial_terms = expert_terms(
        lax.all_gather(local_rows, "dp", axis=0, tiled=True), weights
    ).astype(jnp.bfloat16)
    summed = (
        lax.psum_scatter(partial_terms, "dp", scatter_dimension=0, tiled=True)
        .astype(jnp.float32)
        .astype(jnp.bfloat16)
    )
    result = lax.all_to_all(
        summed.reshape(1, slot_count, models, model_width),
        "expert",
        split_axis=3,
        concat_axis=0,
        tiled=True,
    )
    return result


def per_device(
    policy_hidden,
    reference_hidden,
    policy_norm_gain,
    reference_norm_gain,
    policy_router,
    reference_router,
    policy_gate,
    policy_up,
    policy_down,
    reference_gate,
    reference_up,
    reference_down,
    expert_ids,
    lengths,
):
    expert_count = lax.axis_size("expert")
    token_count, feature_block = policy_hidden.shape
    route_count = expert_ids.shape[1]
    slot_count = 3 * token_count // expert_count
    token_total = float(token_count * lax.axis_size("dp"))
    policy_partial, policy_squares = router_terms(policy_hidden, policy_norm_gain, policy_router)
    reference_partial, reference_squares = router_terms(
        reference_hidden, reference_norm_gain, reference_router
    )
    policy_partial, reference_partial, policy_squares, reference_squares = lax.psum(
        (policy_partial, reference_partial, policy_squares, reference_squares), "expert"
    )
    policy_scale = lax.rsqrt(policy_squares / D + EPSILON)[:, None]
    reference_scale = lax.rsqrt(reference_squares / D + EPSILON)[:, None]
    policy_logits = policy_partial * policy_scale
    reference_logits = reference_partial * reference_scale
    policy_rows = (policy_hidden.astype(jnp.float32) * policy_norm_gain * policy_scale).astype(
        jnp.bfloat16
    )
    reference_rows = (
        reference_hidden.astype(jnp.float32) * reference_norm_gain * reference_scale
    ).astype(jnp.bfloat16)
    live_mask = (
        (jnp.arange(SEG, dtype=jnp.int32)[None, :] < lengths[:, None])
        .reshape(-1)
        .astype(jnp.float32)
    )
    flat_ids = expert_ids.reshape(-1)
    onehot = (flat_ids[:, None] == jnp.arange(expert_count, dtype=jnp.int32)[None, :]).astype(
        jnp.int32
    )
    before = jnp.cumsum(onehot, axis=0) - onehot
    target = flat_ids * slot_count + jnp.sum(before * onehot, axis=1)
    slot_index = jnp.arange(expert_count * slot_count, dtype=jnp.int32)
    select = jnp.any(
        slot_index[:, None, None] == target.reshape(token_count, route_count)[None, :, :], axis=2
    ).astype(jnp.bfloat16)

    def pair_gates(logits):
        matches = expert_ids[:, :, None] == jnp.arange(expert_count, dtype=jnp.int32)[None, None, :]
        chosen = jnp.sum(jnp.where(matches, logits[:, None, :], 0.0), axis=2)
        return jax.nn.softmax(chosen, axis=1)

    def combine(expert_output, gates):
        picked = jnp.take(
            expert_output.reshape(expert_count * slot_count, feature_block), target, axis=0
        )
        picked = picked.reshape(token_count, route_count, feature_block).astype(jnp.float32)
        mixed_rows = jnp.sum(picked * gates[:, :, None], axis=1) * live_mask[:, None]
        return mixed_rows.astype(jnp.bfloat16)

    policy_gate_full, policy_up_full, reference_gate_full, reference_up_full = (
        lax.all_to_all(policy_gate, "dp", split_axis=2, concat_axis=1, tiled=True),
        lax.all_to_all(policy_up, "dp", split_axis=2, concat_axis=1, tiled=True),
        lax.all_to_all(reference_gate, "dp", split_axis=2, concat_axis=1, tiled=True),
        lax.all_to_all(reference_up, "dp", split_axis=2, concat_axis=1, tiled=True),
    )
    stacked_rows = jnp.concatenate((policy_rows, reference_rows), axis=1)
    placed = jnp.dot(select, stacked_rows, preferred_element_type=jnp.float32).astype(jnp.bfloat16)
    expert_output = mixture(
        placed.reshape(expert_count, slot_count, 2, feature_block),
        (
            (policy_gate_full[0], policy_up_full[0], policy_down[0]),
            (reference_gate_full[0], reference_up_full[0], reference_down[0]),
        ),
    )
    policy_output = expert_output[:, :, 0, :]
    reference_output = expert_output[:, :, 1, :]
    policy_mixture = combine(policy_output, pair_gates(policy_logits))
    reference_mixture = combine(reference_output, pair_gates(reference_logits))
    policy_logprob = jax.nn.log_softmax(policy_logits, axis=1)
    reference_logprob = jax.nn.log_softmax(reference_logits, axis=1)
    policy_prob = jnp.exp(policy_logprob)
    token_kl = jnp.sum(policy_prob * (policy_logprob - reference_logprob), axis=1) * live_mask
    route_onehot = onehot.reshape(token_count, route_count, expert_count)
    counts = jnp.sum(jnp.sum(route_onehot, axis=1).astype(jnp.float32) * live_mask[:, None], axis=0)
    probsum = jnp.sum(policy_prob * live_mask[:, None], axis=0)
    counts, probsum, kl_total = lax.psum((counts, probsum, jnp.sum(token_kl)), "dp")
    balance = expert_count * jnp.sum(counts / (route_count * token_total) * probsum / token_total)
    loss = KL_WEIGHT * kl_total / token_total + BALANCE_WEIGHT * balance
    return (policy_mixture, reference_mixture, token_kl, loss)


def solution(mesh):
    in_specs = (
        P("dp", "expert"),
        P("dp", "expert"),
        P("expert"),
        P("expert"),
        P("expert", None),
        P("expert", None),
        P("expert", "dp", None),
        P("expert", "dp", None),
        P("expert", "dp", None),
        P("expert", "dp", None),
        P("expert", "dp", None),
        P("expert", "dp", None),
        P("dp", None),
        P("dp"),
    )
    out_specs = (P("dp", "expert"), P("dp", "expert"), P("dp"), P())
    return jax.shard_map(
        per_device, mesh=mesh, in_specs=in_specs, out_specs=out_specs, check_vma=False
    )
```

profile of v0, /device:TPU:0, one launch (start us, length us, event | category | flops | bytes accessed | tf_op | source)
XLA Modules:
  0.0 886.3 jit_solution(8897518437984197567)
XLA Ops:
  11.9 1.5 fusion.22
  13.4 14.3 %all-reduce.1 = (f32[128]{0:T(128)S(1)}, f32[128]{0:T(128)S(1)}, f32[128,4]{0,1:T(4,128)}, f32[128,4]{0,1:T(4,128)}) all-reduce(f32[128]{0:T(128)S(1)} %fusion.27, f32[128]{0:T(128)S(1)} %fusion.26, f32[128,4]{0,1:T(4,128)S(1)} %fusion.22, f32[128,4]{0,1:T(4,128)S(1)} %fusion.20), channel_id=1, replica_groups=mesh['dp'=8,'expert'=4] {'expert'}, use_global_device_ids=true, to_apply=%region_7.8 | all-reduce | flops 1280 | bytes 10240 | tf_op jit(solution)/shard_map/psum | solution.py:79
  34.2 1.7 copy.105
  35.9 3.6 all-to-all-start
  39.5 34.5 %copy.109 = bf16[1,512,8192]{1,0,2:T(2,128)(2,1)} copy(bf16[1,512,8192]{2,1,0:T(8,128)(2,1)} %param.24) | data formatting | bytes 16777216 | tf_op args[7]
  74.5 54.6 %reduce.6 = bf16[8192,512]{1,0:T(8,128)(2,1)} reduce(bf16[8192,1,512]{2,1,0:T(2,128)(2,1)} %bitcast.98, bf16[]{:T(256)} %broadcast.143), dimensions={1}, to_apply=%bitcast.81.reduce_sub_computation | reduce | bytes 16777218
  129.1 11.2 %reshape.201 = bf16[8,2,262144]{2,1,0:T(2,128)(2,1)} reshape(bf16[8192,512]{1,0:T(8,128)(2,1)} %reduce.6) | data formatting | bytes 16777216
  140.2 5.2 all-to-all-start.2
  145.4 34.5 %copy.107 = bf16[1,512,8192]{1,0,2:T(2,128)(2,1)} copy(bf16[1,512,8192]{2,1,0:T(8,128)(2,1)} %param.23) | data formatting | bytes 16777216 | tf_op args[6]
  180.0 54.6 %reduce.7 = bf16[8192,512]{1,0:T(8,128)(2,1)} reduce(bf16[8192,1,512]{2,1,0:T(2,128)(2,1)} %bitcast.100, bf16[]{:T(256)} %broadcast.143), dimensions={1}, to_apply=%bitcast.83.reduce_sub_computation | reduce | bytes 16777218
  234.6 11.2 %reshape.203 = bf16[8,2,262144]{2,1,0:T(2,128)(2,1)} reshape(bf16[8192,512]{1,0:T(8,128)(2,1)} %reduce.7) | data formatting | bytes 16777216
  245.8 4.9 all-to-all-start.1
  252.0 2.4 reshape.171
  254.4 34.7 %copy.113 = bf16[1,512,8192]{1,0,2:T(2,128)(2,1)} copy(bf16[1,512,8192]{2,1,0:T(8,128)(2,1)} %param.27) | data formatting | bytes 16777216 | tf_op args[10]
  289.2 54.6 %reduce.4 = bf16[8192,512]{1,0:T(8,128)(2,1)} reduce(bf16[8192,1,512]{2,1,0:T(2,128)(2,1)} %bitcast.101, bf16[]{:T(256)} %broadcast.143), dimensions={1}, to_apply=%bitcast.77.reduce_sub_computation | reduce | bytes 16777218
  343.7 11.2 %reshape.197 = bf16[8,2,262144]{2,1,0:T(2,128)(2,1)} reshape(bf16[8192,512]{1,0:T(8,128)(2,1)} %reduce.4) | data formatting | bytes 16777216
  354.9 36.7 %all-to-all-done.1 = bf16[8,2,262144]{2,1,0:T(2,128)(2,1)} async-done(((bf16[8,2,262144]{2,1,0:T(2,128)(2,1)}), bf16[8,2,262144]{2,1,0:T(2,128)(2,1)}, u32[]{:S(2)}, u32[]{:S(2)}) %all-to-all-start.1) | async-done | bytes 8388640 | tf_op jit(solution)/shard_map/all_to_all | solution.py:122
  391.6 5.4 all-to-all-start.4
  397.0 34.5 %copy.111 = bf16[1,512,8192]{1,0,2:T(2,128)(2,1)} copy(bf16[1,512,8192]{2,1,0:T(8,128)(2,1)} %param.26) | data formatting | bytes 16777216 | tf_op args[9]
  431.5 54.6 %reduce.5 = bf16[8192,512]{1,0:T(8,128)(2,1)} reduce(bf16[8192,1,512]{2,1,0:T(2,128)(2,1)} %bitcast.99, bf16[]{:T(256)} %broadcast.143), dimensions={1}, to_apply=%bitcast.79.reduce_sub_computation | reduce | bytes 16777218
  486.1 11.2 %reshape.199 = bf16[8,2,262144]{2,1,0:T(2,128)(2,1)} reshape(bf16[8192,512]{1,0:T(8,128)(2,1)} %reduce.5) | data formatting | bytes 16777216
  497.3 4.9 all-to-all-start.3
  502.3 13.3 %reshape.202 = bf16[8192,1,512]{2,1,0:T(2,128)(2,1)} reshape(bf16[8,2,262144]{2,1,0:T(2,128)(2,1)} %all-to-all-done.2) | data formatting | bytes 16777216
  515.6 11.6 %copy.120 = bf16[1,512,8192]{1,2,0:T(8,128)(2,1)} copy(bf16[1,512,8192]{1,0,2:T(2,128)(2,1)} %bitcast.94) | data formatting | bytes 16777216
  527.2 11.4 %copy.110 = bf16[1,8,512,1024]{3,2,1,0:T(8,128)(2,1)} copy(bf16[1,8,512,1024]{2,3,1,0:T(8,128)(2,1)} %bitcast.102) | data formatting | bytes 16777216 | tf_op jit(solution)/shard_map/all_to_all | solution.py:123
  538.7 13.3 %reshape.204 = bf16[8192,1,512]{2,1,0:T(2,128)(2,1)} reshape(bf16[8,2,262144]{2,1,0:T(2,128)(2,1)} %all-to-all-done.1) | data formatting | bytes 16777216
  552.0 11.6 %copy.119 = bf16[1,512,8192]{1,2,0:T(8,128)(2,1)} copy(bf16[1,512,8192]{1,0,2:T(2,128)(2,1)} %bitcast.95) | data formatting | bytes 16777216
  563.6 11.4 %copy.108 = bf16[1,8,512,1024]{3,2,1,0:T(8,128)(2,1)} copy(bf16[1,8,512,1024]{2,3,1,0:T(8,128)(2,1)} %bitcast.103) | data formatting | bytes 16777216 | tf_op jit(solution)/shard_map/all_to_all | solution.py:122
  575.0 13.3 %reshape.198 = bf16[8192,1,512]{2,1,0:T(2,128)(2,1)} reshape(bf16[8,2,262144]{2,1,0:T(2,128)(2,1)} %all-to-all-done.4) | data formatting | bytes 16777216
  588.3 11.6 %copy.122 = bf16[1,512,8192]{1,2,0:T(8,128)(2,1)} copy(bf16[1,512,8192]{1,0,2:T(2,128)(2,1)} %bitcast.96) | data formatting | bytes 16777216
  600.0 11.5 %copy.114 = bf16[1,8,512,1024]{3,2,1,0:T(8,128)(2,1)} copy(bf16[1,8,512,1024]{2,3,1,0:T(8,128)(2,1)} %bitcast.104) | data formatting | bytes 16777216 | tf_op jit(solution)/shard_map/all_to_all | solution.py:125
  611.4 13.3 %reshape.200 = bf16[8192,1,512]{2,1,0:T(2,128)(2,1)} reshape(bf16[8,2,262144]{2,1,0:T(2,128)(2,1)} %all-to-all-done.3) | data formatting | bytes 16777216
  624.7 11.8 %copy.121 = bf16[1,512,8192]{1,2,0:T(8,128)(2,1)} copy(bf16[1,512,8192]{1,0,2:T(2,128)(2,1)} %bitcast.97) | data formatting | bytes 16777216
  636.6 11.5 %copy.112 = bf16[1,8,512,1024]{3,2,1,0:T(8,128)(2,1)} copy(bf16[1,8,512,1024]{2,3,1,0:T(8,128)(2,1)} %bitcast.105) | data formatting | bytes 16777216 | tf_op jit(solution)/shard_map/all_to_all | solution.py:124
  648.0 11.0 %fusion.16 = f32[768,1024]{1,0:T(8,128)S(1)} fusion(bf16[4096,1024]{1,0:T(8,128)(2,1)} %bitcast.109, bf16[768,2,4096]{2,0,1:T(8,128)(2,1)} %all-gather.2.cloned.1.call-done), kind=kOutput, calls=%fused_computation.13 | convolution fusion | flops 6442450944 | bytes 17825792 | tf_op jit(solution)/shard_map/dot_general | solution.py:25
  659.1 9.7 %multiply_convert_fusion.1 = bf16[768,1024]{1,0:T(8,128)(2,1)S(1)} fusion(f32[768,1024]{1,0:T(8,128)S(1)} %fusion.16, bf16[4096,1024]{1,0:T(8,128)(2,1)} %bitcast.110, bf16[768,2,4096]{2,0,1:T(8,128)(2,1)S(1)} %copy-done.13), kind=kOutput, calls=%fused_computation.18 | convolution fusion | flops 6447169536 | bytes 19398656 | tf_op jit(solution)/shard_map/dot_general | solution.py:24
  668.8 10.6 %fusion.13 = bf16[768,1,4096]{2,0,1:T(8,128)(2,1)S(1)} fusion(bf16[768,1024]{1,0:T(8,128)(2,1)S(1)} %multiply_convert_fusion.1, bf16[1,1024,4096]{2,1,0:T(8,128)(2,1)} %param.25), kind=kOutput, calls=%fused_computation.12 | convolution fusion | flops 6445596672 | bytes 16252928 | tf_op jit(solution)/shard_map/dot_general | solution.py:27
  679.5 10.2 %fusion.18 = f32[768,1024]{1,0:T(8,128)} fusion(bf16[4096,1024]{1,0:T(8,128)(2,1)S(1)} %bitcast.113, bf16[768,2,4096]{2,0,1:T(8,128)(2,1)} %all-gather.2.cloned.1.call-done), kind=kOutput, calls=%fused_computation.15 | convolution fusion | flops 6442450944 | bytes 17825792 | tf_op jit(solution)/shard_map/dot_general | solution.py:25
  689.7 10.0 %multiply_convert_fusion = bf16[768,1024]{1,0:T(8,128)(2,1)S(1)} fusion(f32[768,1024]{1,0:T(8,128)} %fusion.18, bf16[4096,1024]{1,0:T(8,128)(2,1)S(1)} %bitcast.116, bf16[768,2,4096]{2,0,1:T(8,128)(2,1)} %all-gather.2.cloned.1.call-done), kind=kOutput, calls=%fused_computation.17 | convolution fusion | flops 6447169536 | bytes 19398656 | tf_op jit(solution)/shard_map/dot_general | solution.py:24
  699.7 7.3 fusion.10
  707.0 5.4 pad_maximum_fusion
  712.5 94.5 %reduce-scatter.2.cloned.1.call-done = bf16[96,2,4096]{2,0,1:T(8,128)(2,1)} async-done(((bf16[768,2,4096]{2,0,1:T(8,128)(2,1)}), bf16[96,2,4096]{2,0,1:T(8,128)(2,1)}) %reduce-scatter.2.cloned.1.call-update) | async-done | bytes 1572880 | tf_op jit(solution)/shard_map/reduce_scatter | solution.py:40
  807.0 5.7 copy.115
  812.7 4.6 all-to-all-start.5
  818.9 13.4 %all-reduce = (f32[]{:T(128)}, f32[4]{0:T(128)S(1)}, f32[4]{0:T(128)S(1)}) all-reduce(f32[]{:T(128)} %get-tuple-element.18, f32[4]{0:T(128)S(1)} %get-tuple-element.6, f32[4]{0:T(128)S(1)} %get-tuple-element.10), channel_id=1, replica_groups=mesh['dp'=8,'expert'=4] {'dp'}, use_global_device_ids=true, to_apply=%region_23.26 | all-reduce | flops 9 | bytes 72 | tf_op jit(solution)/shard_map/psum | solution.py:147
  834.7 30.7 %all-to-all-done.5 = bf16[1,96,2,4096]{1,2,0,3:T(2,128)(2,1)S(1)} async-done(((bf16[1,96,2,4096]{1,2,0,3:T(2,128)(2,1)}), bf16[1,96,2,4096]{1,2,0,3:T(2,128)(2,1)S(1)}, u32[]{:S(2)}, u32[]{:S(2)}) %all-to-all-start.5) | async-done | bytes 1572896 | tf_op jit(solution)/shard_map/all_to_all | solution.py:44
  865.4 3.7 copy.116
  869.1 1.6 fusion.47
  (112 shorter events, 23.1 us)
Async XLA Ops:
  7.2 3.3 copy-start
  8.3 24.2 %copy-start.3 = (s32[256]{0:T(256)}, s32[256]{0:T(256)S(1)}, u32[]{:S(2)}) copy-start(s32[256]{0:T(256)S(1)} %eq.60) | copy-start | bytes 3076
  27.7 1.1 copy-start.9
  27.7 2.1 copy-start.7
  31.5 42.5 %copy-start.5 = (s32[256]{0:T(256)}, s32[256]{0:T(256)S(1)}, u32[]{:S(2)}) copy-start(s32[256]{0:T(256)S(1)} %fusion.36) | copy-start | bytes 3076
  35.9 104.3 %all-to-all-start = ((bf16[4,96,2,1024]{3,1,2,0:T(8,128)(2,1)}), bf16[4,96,2,1024]{3,1,2,0:T(8,128)(2,1)S(1)}, u32[]{:S(2)}, u32[]{:S(2)}) async-start(bf16[4,96,2,1024]{3,1,2,0:T(8,128)(2,1)} %copy.105), calls=%async_computation | async-start | bytes 3145728 | tf_op jit(solution)/shard_map/all_to_all | solution.py:34
  140.2 105.5 %all-to-all-start.2 = ((bf16[8,2,262144]{2,1,0:T(2,128)(2,1)}), bf16[8,2,262144]{2,1,0:T(2,128)(2,1)}, u32[]{:S(2)}, u32[]{:S(2)}) async-start(bf16[8,2,262144]{2,1,0:T(2,128)(2,1)} %reshape.201), calls=%async_computation.2 | async-start | bytes 16777216 | tf_op jit(solution)/shard_map/all_to_all | solution.py:123
  245.8 145.8 %all-to-all-start.1 = ((bf16[8,2,262144]{2,1,0:T(2,128)(2,1)}), bf16[8,2,262144]{2,1,0:T(2,128)(2,1)}, u32[]{:S(2)}, u32[]{:S(2)}) async-start(bf16[8,2,262144]{2,1,0:T(2,128)(2,1)} %reshape.203), calls=%async_computation.1 | async-start | bytes 16777216 | tf_op jit(solution)/shard_map/all_to_all | solution.py:122
  250.7 397.3 %all-gather.2.cloned.1.call-start = ((), (), s32[]{:S(2)}) async-start(), calls=%async_computation.7 | async-start | bytes 14155776 | tf_op jit(solution)/shard_map/all_gather | solution.py:37
  391.6 105.7 %all-to-all-start.4 = ((bf16[8,2,262144]{2,1,0:T(2,128)(2,1)}), bf16[8,2,262144]{2,1,0:T(2,128)(2,1)}, u32[]{:S(2)}, u32[]{:S(2)}) async-start(bf16[8,2,262144]{2,1,0:T(2,128)(2,1)} %reshape.197), calls=%async_computation.4 | async-start | bytes 16777216 | tf_op jit(solution)/shard_map/all_to_all | solution.py:125
  497.3 114.2 %all-to-all-start.3 = ((bf16[8,2,262144]{2,1,0:T(2,128)(2,1)}), bf16[8,2,262144]{2,1,0:T(2,128)(2,1)}, u32[]{:S(2)}, u32[]{:S(2)}) async-start(bf16[8,2,262144]{2,1,0:T(2,128)(2,1)} %reshape.199), calls=%async_computation.3 | async-start | bytes 16777216 | tf_op jit(solution)/shard_map/all_to_all | solution.py:124
  502.2 304.8 %reduce-scatter.2.cloned.1.call-start = ((), (), s32[]{:S(2)}) async-start(), calls=%async_computation.8 | async-start | bytes 14155776 | tf_op jit(solution)/shard_map/reduce_scatter | solution.py:40
  648.0 11.0 %copy-start.13 = (bf16[768,2,4096]{2,0,1:T(8,128)(2,1)S(1)}, bf16[768,2,4096]{2,0,1:T(8,128)(2,1)}, u32[]{:S(2)}) copy-start(bf16[768,2,4096]{2,0,1:T(8,128)(2,1)} %all-gather.2.cloned.1.call-done) | copy-start | bytes 37748740
  659.1 20.4 %slice-start = ((s8[8388608]{0:T(1024)(128)(4,1)}), s8[4194304]{0:T(1024)(128)(4,1)S(1)}, s32[]{:S(2)}) async-start(s8[8388608]{0:T(1024)(128)(4,1)} %bitcast.111), calls=%async_computation.9 | async-start | bytes 8388608
  668.8 10.7 %slice-start.1 = ((s8[8388608]{0:T(1024)(128)(4,1)}), s8[4194304]{0:T(1024)(128)(4,1)S(1)}, s32[]{:S(2)}) async-start(s8[8388608]{0:T(1024)(128)(4,1)} %bitcast.111), calls=%async_computation.10 | async-start | bytes 8388608
  668.8 20.9 %slice-start.2 = ((s8[8388608]{0:T(1024)(128)(4,1)}), s8[4194304]{0:T(1024)(128)(4,1)S(1)}, s32[]{:S(2)}) async-start(s8[8388608]{0:T(1024)(128)(4,1)} %bitcast.114), calls=%async_computation.11 | async-start | bytes 8388608
  668.8 30.9 %slice-start.4 = ((s8[8388608]{0:T(1024)(128)(4,1)}), s8[4194304]{0:T(1024)(128)(4,1)S(1)}, s32[]{:S(2)}) async-start(s8[8388608]{0:T(1024)(128)(4,1)} %bitcast.121), calls=%async_computation.13 | async-start | bytes 8388608
  679.5 10.2 %slice-start.3 = ((s8[8388608]{0:T(1024)(128)(4,1)}), s8[4194304]{0:T(1024)(128)(4,1)S(1)}, s32[]{:S(2)}) async-start(s8[8388608]{0:T(1024)(128)(4,1)} %bitcast.114), calls=%async_computation.12 | async-start | bytes 8388608
  679.5 20.2 %slice-start.5 = ((s8[8388608]{0:T(1024)(128)(4,1)}), s8[4194304]{0:T(1024)(128)(4,1)S(1)}, s32[]{:S(2)}) async-start(s8[8388608]{0:T(1024)(128)(4,1)} %bitcast.121), calls=%async_computation.14 | async-start | bytes 8388608
  712.4 104.9 %copy-start.14 = (s32[4]{0:T(128)S(1)}, s32[4]{0:T(128)}, u32[]{:S(2)}) copy-start(s32[4]{0:T(128)} %param.30) | copy-start | bytes 52
  712.4 105.1 %copy-start.10 = (f32[128]{0:T(128)S(1)}, f32[128]{0:T(128)}, u32[]{:S(2)}) copy-start(f32[128]{0:T(128)} %copy-done.9) | copy-start | bytes 1540
  712.4 105.1 %copy-start.12 = (f32[128,4]{0,1:T(4,128)S(1)}, f32[128,4]{0,1:T(4,128)}, u32[]{:S(2)}) copy-start(f32[128,4]{0,1:T(4,128)} %get-tuple-element.16) | copy-start | bytes 6148
  712.4 105.1 %copy-start.8 = (f32[128]{0:T(128)S(1)}, f32[128]{0:T(128)}, u32[]{:S(2)}) copy-start(f32[128]{0:T(128)} %copy-done.7) | copy-start | bytes 1540
  712.4 105.1 %copy-start.11 = (f32[128,4]{0,1:T(4,128)S(1)}, f32[128,4]{0,1:T(4,128)}, u32[]{:S(2)}) copy-start(f32[128,4]{0,1:T(4,128)} %get-tuple-element.17) | copy-start | bytes 6148
  712.4 105.2 %copy-start.2 = (s32[128,2]{0,1:T(2,128)S(1)}, s32[128,2]{0,1:T(2,128)}, u32[]{:S(2)}) copy-start(s32[128,2]{0,1:T(2,128)} %param.29) | copy-start | bytes 3076
  712.4 122.2 %copy-start.4 = (s32[256]{0:T(256)S(1)}, s32[256]{0:T(256)}, u32[]{:S(2)}) copy-start(s32[256]{0:T(256)} %copy-done.3) | copy-start | bytes 3076
  712.5 122.2 %copy-start.6 = (s32[256]{0:T(256)S(1)}, s32[256]{0:T(256)}, u32[]{:S(2)}) copy-start(s32[256]{0:T(256)} %copy-done.5) | copy-start | bytes 3076
  812.7 52.6 %all-to-all-start.5 = ((bf16[1,96,2,4096]{1,2,0,3:T(2,128)(2,1)}), bf16[1,96,2,4096]{1,2,0,3:T(2,128)(2,1)S(1)}, u32[]{:S(2)}, u32[]{:S(2)}) async-start(bf16[1,96,2,4096]{1,2,0,3:T(2,128)(2,1)} %copy.115), calls=%async_computation.6 | async-start | bytes 4194304 | tf_op jit(solution)/shard_map/all_to_all | solution.py:44
  871.8 6.3 copy-start.1
Sparse Core Ops, SparseCore 0:
  254.6 141.9 all-gather.1
  712.6 94.3 reduce-scatter.1
where the time goes:
time: 900 us; the launch traced here: 886 us
  local copies, waits for them, and re-layouts  352 us (39%)
  other arithmetic  236 us (26%)
  waiting for transfers between devices  162 us (18%)
  matrix products  62.3 us (7%)
  starting transfers between devices  28.7 us (3%)
  blocking collectives  27.7 us (3%)
  between operations  17.2 us (2%)
    unnamed x60, local copies, waits for them, and re-layouts  284 us
    unnamed x8, other arithmetic  218 us
    reduce_scatter x1, waiting for transfers between devices, mixture(): lax.psum_scatter(partial_terms, 'dp', scatter_dimension=0, tiled=True)  94.5 us
    all_to_all x1, waiting for transfers between devices, per_device(): lax.all_to_all(policy_gate, 'dp', split_axis=2, concat_axis=1, tiled=True)  36.7 us
    all_to_all x1, waiting for transfers between devices, mixture(): lax.all_to_all(summed.reshape(1, slot_count, models, model_width), 'exper...  30.7 us
    dot_general x2, matrix products, expert_terms(): jnp.dot(model_rows, up_weight, preferred_element_type=jnp.float32)  21.2 us
    dot_general x2, matrix products, expert_terms(): jnp.dot(model_rows, gate_weight, preferred_element_type=jnp.float32)  19.7 us
  transfers between devices with their start and end apart: 8, of which 3 were waited for; matrix products, arithmetic and copies ran while one was open for 62% of the time, Pallas kernels for 0%

commit v1 on v0

--- a/solution.py
+++ b/solution.py
@@ -119,7 +119,12 @@
         return mixed_rows.astype(jnp.bfloat16)
 
     policy_gate_full, policy_up_full, reference_gate_full, reference_up_full = (
-        lax.all_to_all(policy_gate, "dp", split_axis=2, concat_axis=1, tiled=True),
+        jnp.concatenate(
+            lax.all_to_all(
+                jnp.stack(jnp.split(policy_gate, lax.axis_size("dp"), axis=2)), "dp", 0, 0
+            ),
+            axis=1,
+        ),
         lax.all_to_all(policy_up, "dp", split_axis=2, concat_axis=1, tiled=True),
         lax.all_to_all(reference_gate, "dp", split_axis=2, concat_axis=1, tiled=True),
         lax.all_to_all(reference_up, "dp", split_axis=2, concat_axis=1, tiled=True),

time: 900 us -> 859 us (0.954)
  waiting for transfers between devices: 162 us -> 237 us
  local copies, waits for them, and re-layouts: 352 us -> 288 us
  other arithmetic: 236 us -> 182 us
    all_to_all x1, waiting for transfers between devices: 0.01 us -> 75.7 us  [per_device(): lax.all_to_all(policy_up, 'dp', split_axis=2, concat_axis=1, tiled=True)]
    unnamed x60 -> x59, local copies, waits for them, and re-layouts: 284 us -> 230 us
    unnamed x8 -> x6, other arithmetic: 218 us -> 164 us
    all_to_all x1, waiting for transfers between devices: 36.7 us -> 0.01 us  [per_device(): lax.all_to_all(jnp.stack(jnp.split(policy_gate, lax.axis_size('dp'), axis...]
    all_to_all x1, waiting for transfers between devices: 0.01 us -> 36.4 us  [per_device(): lax.all_to_all(reference_up, 'dp', split_axis=2, concat_axis=1, tiled=True)]
    all_to_all x1 -> x0, local copies, waits for them, and re-layouts: 11.4 us -> none  [per_device(): lax.all_to_all(policy_gate, 'dp', split_axis=2, concat_axis=1, tiled=True)]
  transfers between devices with their start and end apart: 8 -> 8, of which waited for: 3 -> 4; matrix products, arithmetic and copies ran while one was open for 62% -> 56% of each run, Pallas kernels for 0% -> 0%
where the time goes in v1:
time: 859 us; the launch traced here: 846 us
  local copies, waits for them, and re-layouts  288 us (34%)
  waiting for transfers between devices  237 us (28%)
  other arithmetic  182 us (21%)
  matrix products  65.8 us (8%)
  starting transfers between devices  28.5 us (3%)
  blocking collectives  27.7 us (3%)
  between operations  17.1 us (2%)
    unnamed x59, local copies, waits for them, and re-layouts  230 us
    unnamed x6, other arithmetic  164 us
    reduce_scatter x1, waiting for transfers between devices, mixture(): lax.psum_scatter(partial_terms, 'dp', scatter_dimension=0, tiled=True)  94.5 us
    all_to_all x1, waiting for transfers between devices, per_device(): lax.all_to_all(policy_up, 'dp', split_axis=2, concat_axis=1, tiled=True)  75.7 us
    all_to_all x1, waiting for transfers between devices, per_device(): lax.all_to_all(reference_up, 'dp', split_axis=2, concat_axis=1, tiled=True)  36.4 us
    all_to_all x1, waiting for transfers between devices, mixture(): lax.all_to_all(summed.reshape(1, slot_count, models, model_width), 'exper...  30.6 us
    dot_general x2, matrix products, expert_terms(): jnp.dot(hidden, down_weight, preferred_element_type=jnp.float32)  22.9 us
    dot_general x2, matrix products, expert_terms(): jnp.dot(model_rows, gate_weight, preferred_element_type=jnp.float32)  21.7 us
  transfers between devices with their start and end apart: 8, of which 4 were waited for; matrix products, arithmetic and copies ran while one was open for 56% of the time, Pallas kernels for 0%

profile of v1, /device:TPU:0, one launch (start us, length us, event | category | flops | bytes accessed | tf_op | source)
XLA Modules:
  0.0 846.2 jit_solution(1451613363071750666)
XLA Ops:
  13.4 14.3 %all-reduce.1 = (f32[128]{0:T(128)S(1)}, f32[128]{0:T(128)S(1)}, f32[128,4]{0,1:T(4,128)}, f32[128,4]{0,1:T(4,128)}) all-reduce(f32[128]{0:T(128)S(1)} %fusion.27, f32[128]{0:T(128)S(1)} %fusion.26, f32[128,4]{0,1:T(4,128)S(1)} %fusion.22, f32[128,4]{0,1:T(4,128)S(1)} %fusion.20), channel_id=1, replica_groups=mesh['dp'=8,'expert'=4] {'expert'}, use_global_device_ids=true, to_apply=%region_7.8 | all-reduce | flops 1280 | bytes 10240 | tf_op jit(solution)/shard_map/psum | solution.py:79
  35.9 3.6 all-to-all-start
  39.5 34.5 %copy.105 = bf16[1,512,8192]{1,0,2:T(2,128)(2,1)} copy(bf16[1,512,8192]{2,1,0:T(8,128)(2,1)} %param.27) | data formatting | bytes 16777216 | tf_op args[10]
  74.5 54.6 %reduce.4 = bf16[8192,512]{1,0:T(8,128)(2,1)} reduce(bf16[8192,1,512]{2,1,0:T(2,128)(2,1)} %bitcast.108, bf16[]{:T(256)} %broadcast.143), dimensions={1}, to_apply=%bitcast.90.reduce_sub_computation | reduce | bytes 16777218
  129.1 11.2 %reshape.196 = bf16[8,2,262144]{2,1,0:T(2,128)(2,1)} reshape(bf16[8192,512]{1,0:T(8,128)(2,1)} %reduce.4) | data formatting | bytes 16777216
  140.2 5.0 all-to-all-start.4
  146.7 2.4 reshape.170
  149.2 34.7 %copy.103 = bf16[1,512,8192]{1,0,2:T(2,128)(2,1)} copy(bf16[1,512,8192]{2,1,0:T(8,128)(2,1)} %param.26) | data formatting | bytes 16777216 | tf_op args[9]
  183.9 54.6 %reduce.5 = bf16[8192,512]{1,0:T(8,128)(2,1)} reduce(bf16[8192,1,512]{2,1,0:T(2,128)(2,1)} %bitcast.110, bf16[]{:T(256)} %broadcast.143), dimensions={1}, to_apply=%bitcast.92.reduce_sub_computation | reduce | bytes 16777218
  238.5 11.2 %reshape.198 = bf16[8,2,262144]{2,1,0:T(2,128)(2,1)} reshape(bf16[8192,512]{1,0:T(8,128)(2,1)} %reduce.5) | data formatting | bytes 16777216
  249.7 36.4 %all-to-all-done.4 = bf16[8,2,262144]{2,1,0:T(2,128)(2,1)} async-done(((bf16[8,2,262144]{2,1,0:T(2,128)(2,1)}), bf16[8,2,262144]{2,1,0:T(2,128)(2,1)}, u32[]{:S(2)}, u32[]{:S(2)}) %all-to-all-start.4) | async-done | bytes 8388640 | tf_op jit(solution)/shard_map/all_to_all | solution.py:130
  286.1 4.9 all-to-all-start.3
  291.0 34.5 %copy.101 = bf16[1,512,8192]{1,0,2:T(2,128)(2,1)} copy(bf16[1,512,8192]{2,1,0:T(8,128)(2,1)} %param.24) | data formatting | bytes 16777216 | tf_op args[7]
  325.6 54.6 %reduce.6 = bf16[8192,512]{1,0:T(8,128)(2,1)} reduce(bf16[8192,1,512]{2,1,0:T(2,128)(2,1)} %bitcast.109, bf16[]{:T(256)} %broadcast.143), dimensions={1}, to_apply=%bitcast.94.reduce_sub_computation | reduce | bytes 16777218
  380.2 11.2 %reshape.200 = bf16[8,2,262144]{2,1,0:T(2,128)(2,1)} reshape(bf16[8192,512]{1,0:T(8,128)(2,1)} %reduce.6) | data formatting | bytes 16777216
  391.3 5.0 all-to-all-start.2
  396.3 2.3 bitcast_dynamic-update-slice_fusion.7
  398.6 2.3 bitcast_dynamic-update-slice_fusion.6
  400.9 2.3 bitcast_dynamic-update-slice_fusion.5
  403.2 2.3 bitcast_dynamic-update-slice_fusion.4
  405.4 2.3 bitcast_dynamic-update-slice_fusion.3
  407.8 2.3 bitcast_dynamic-update-slice_fusion.2
  410.1 2.3 bitcast_dynamic-update-slice_fusion.1
  412.3 2.3 bitcast_dynamic-update-slice_fusion
  414.6 75.7 %all-to-all-done.2 = bf16[8,2,262144]{2,1,0:T(2,128)(2,1)} async-done(((bf16[8,2,262144]{2,1,0:T(2,128)(2,1)}), bf16[8,2,262144]{2,1,0:T(2,128)(2,1)}, u32[]{:S(2)}, u32[]{:S(2)}) %all-to-all-start.2) | async-done | bytes 8388640 | tf_op jit(solution)/shard_map/all_to_all | solution.py:128
  490.3 5.1 all-to-all-start.1
  495.5 13.3 %reshape.197 = bf16[8192,1,512]{2,1,0:T(2,128)(2,1)} reshape(bf16[8,2,262144]{2,1,0:T(2,128)(2,1)} %all-to-all-done.4) | data formatting | bytes 16777216
  508.8 11.6 %copy.113 = bf16[1,512,8192]{1,2,0:T(8,128)(2,1)} copy(bf16[1,512,8192]{1,0,2:T(2,128)(2,1)} %bitcast.105) | data formatting | bytes 16777216
  520.5 11.4 %copy.106 = bf16[1,8,512,1024]{3,2,1,0:T(8,128)(2,1)} copy(bf16[1,8,512,1024]{2,3,1,0:T(8,128)(2,1)} %bitcast.111) | data formatting | bytes 16777216 | tf_op jit(solution)/shard_map/all_to_all | solution.py:130
  531.9 13.3 %reshape.199 = bf16[8192,1,512]{2,1,0:T(2,128)(2,1)} reshape(bf16[8,2,262144]{2,1,0:T(2,128)(2,1)} %all-to-all-done.3) | data formatting | bytes 16777216
  545.2 11.6 %copy.112 = bf16[1,512,8192]{1,2,0:T(8,128)(2,1)} copy(bf16[1,512,8192]{1,0,2:T(2,128)(2,1)} %bitcast.106) | data formatting | bytes 16777216
  556.9 11.4 %copy.104 = bf16[1,8,512,1024]{3,2,1,0:T(8,128)(2,1)} copy(bf16[1,8,512,1024]{2,3,1,0:T(8,128)(2,1)} %bitcast.112) | data formatting | bytes 16777216 | tf_op jit(solution)/shard_map/all_to_all | solution.py:129
  568.3 13.3 %reshape.201 = bf16[8192,1,512]{2,1,0:T(2,128)(2,1)} reshape(bf16[8,2,262144]{2,1,0:T(2,128)(2,1)} %all-to-all-done.2) | data formatting | bytes 16777216
  581.6 11.6 %copy.111 = bf16[1,512,8192]{1,2,0:T(8,128)(2,1)} copy(bf16[1,512,8192]{1,0,2:T(2,128)(2,1)} %bitcast.107) | data formatting | bytes 16777216
  593.2 11.4 %copy.102 = bf16[1,8,512,1024]{3,2,1,0:T(8,128)(2,1)} copy(bf16[1,8,512,1024]{2,3,1,0:T(8,128)(2,1)} %bitcast.113) | data formatting | bytes 16777216 | tf_op jit(solution)/shard_map/all_to_all | solution.py:128
  604.7 11.0 %fusion.18 = f32[768,1024]{1,0:T(8,128)S(1)} fusion(bf16[4096,1024]{1,0:T(8,128)(2,1)} %bitcast.117, bf16[768,2,4096]{2,0,1:T(8,128)(2,1)} %all-gather.2.cloned.1.call-done), kind=kOutput, calls=%fused_computation.15 | convolution fusion | flops 6442450944 | bytes 17825792 | tf_op jit(solution)/shard_map/dot_general | solution.py:25
  615.8 10.2 %multiply_convert_fusion = bf16[768,1024]{1,0:T(8,128)(2,1)S(1)} fusion(f32[768,1024]{1,0:T(8,128)S(1)} %fusion.18, bf16[4096,1024]{1,0:T(8,128)(2,1)} %bitcast.118, bf16[768,2,4096]{2,0,1:T(8,128)(2,1)S(1)} %copy-done.13), kind=kOutput, calls=%fused_computation.17 | convolution fusion | flops 6447169536 | bytes 19398656 | tf_op jit(solution)/shard_map/dot_general | solution.py:24
  625.9 12.1 %fusion.10 = bf16[768,1,4096]{2,0,1:T(8,128)(2,1)} fusion(bf16[768,1024]{1,0:T(8,128)(2,1)S(1)} %multiply_convert_fusion, bf16[1,1024,4096]{2,1,0:T(8,128)(2,1)} %param.28), kind=kOutput, calls=%fused_computation.11 | convolution fusion | flops 6445596672 | bytes 16252928 | tf_op jit(solution)/shard_map/dot_general | solution.py:27
  638.0 6.7 fusion.16
  644.7 11.5 %multiply_convert_fusion.1 = bf16[768,1024]{1,0:T(8,128)(2,1)S(1)} fusion(f32[768,1024]{1,0:T(8,128)S(1)} %fusion.16, bf16[4096,1024]{1,0:T(8,128)(2,1)} %bitcast.13, bf16[768,2,4096]{2,0,1:T(8,128)(2,1)} %all-gather.2.cloned.1.call-done), kind=kOutput, calls=%fused_computation.18 | convolution fusion | flops 6447169536 | bytes 19398656 | tf_op jit(solution)/shard_map/dot_general | solution.py:24
  656.2 10.8 %fusion.13 = bf16[768,1,4096]{2,0,1:T(8,128)(2,1)S(1)} fusion(bf16[768,1024]{1,0:T(8,128)(2,1)S(1)} %multiply_convert_fusion.1, bf16[1,1024,4096]{2,1,0:T(8,128)(2,1)} %param.25), kind=kOutput, calls=%fused_computation.12 | convolution fusion | flops 6445596672 | bytes 16252928 | tf_op jit(solution)/shard_map/dot_general | solution.py:27
  667.1 5.4 pad_maximum_fusion
  672.6 94.5 %reduce-scatter.2.cloned.1.call-done = bf16[96,2,4096]{2,0,1:T(8,128)(2,1)} async-done(((bf16[768,2,4096]{2,0,1:T(8,128)(2,1)}), bf16[96,2,4096]{2,0,1:T(8,128)(2,1)}) %reduce-scatter.2.cloned.1.call-update) | async-done | bytes 1572880 | tf_op jit(solution)/shard_map/reduce_scatter | solution.py:40
  767.0 5.7 copy.107
  772.7 4.6 all-to-all-start.5
  778.9 13.4 %all-reduce = (f32[]{:T(128)}, f32[4]{0:T(128)S(1)}, f32[4]{0:T(128)S(1)}) all-reduce(f32[]{:T(128)} %get-tuple-element.18, f32[4]{0:T(128)S(1)} %get-tuple-element.6, f32[4]{0:T(128)S(1)} %get-tuple-element.10), channel_id=1, replica_groups=mesh['dp'=8,'expert'=4] {'dp'}, use_global_device_ids=true, to_apply=%region_23.26 | all-reduce | flops 9 | bytes 72 | tf_op jit(solution)/shard_map/psum | solution.py:152
  794.7 30.6 %all-to-all-done.5 = bf16[1,96,2,4096]{1,2,0,3:T(2,128)(2,1)S(1)} async-done(((bf16[1,96,2,4096]{1,2,0,3:T(2,128)(2,1)}), bf16[1,96,2,4096]{1,2,0,3:T(2,128)(2,1)S(1)}, u32[]{:S(2)}, u32[]{:S(2)}) %all-to-all-start.5) | async-done | bytes 1572896 | tf_op jit(solution)/shard_map/all_to_all | solution.py:44
  825.3 3.7 copy.108
  (109 shorter events, 27.9 us)
Async XLA Ops:
  7.2 3.3 copy-start
  8.3 24.2 %copy-start.3 = (s32[256]{0:T(256)}, s32[256]{0:T(256)S(1)}, u32[]{:S(2)}) copy-start(s32[256]{0:T(256)S(1)} %eq.60) | copy-start | bytes 3076
  27.7 1.1 copy-start.9
  27.7 2.1 copy-start.7
  31.5 42.5 %copy-start.5 = (s32[256]{0:T(256)}, s32[256]{0:T(256)S(1)}, u32[]{:S(2)}) copy-start(s32[256]{0:T(256)S(1)} %fusion.36) | copy-start | bytes 3076
  35.9 104.3 %all-to-all-start = ((bf16[4,96,2,1024]{3,1,2,0:T(8,128)(2,1)}), bf16[4,96,2,1024]{3,1,2,0:T(8,128)(2,1)S(1)}, u32[]{:S(2)}, u32[]{:S(2)}) async-start(bf16[4,96,2,1024]{3,1,2,0:T(8,128)(2,1)} %copy.99), calls=%async_computation | async-start | bytes 3145728 | tf_op jit(solution)/shard_map/all_to_all | solution.py:34
  140.2 145.8 %all-to-all-start.4 = ((bf16[8,2,262144]{2,1,0:T(2,128)(2,1)}), bf16[8,2,262144]{2,1,0:T(2,128)(2,1)}, u32[]{:S(2)}, u32[]{:S(2)}) async-start(bf16[8,2,262144]{2,1,0:T(2,128)(2,1)} %reshape.196), calls=%async_computation.4 | async-start | bytes 16777216 | tf_op jit(solution)/shard_map/all_to_all | solution.py:130
  145.3 459.4 %all-gather.2.cloned.1.call-start = ((), (), s32[]{:S(2)}) async-start(), calls=%async_computation.7 | async-start | bytes 14155776 | tf_op jit(solution)/shard_map/all_gather | solution.py:37
  286.1 105.2 %all-to-all-start.3 = ((bf16[8,2,262144]{2,1,0:T(2,128)(2,1)}), bf16[8,2,262144]{2,1,0:T(2,128)(2,1)}, u32[]{:S(2)}, u32[]{:S(2)}) async-start(bf16[8,2,262144]{2,1,0:T(2,128)(2,1)} %reshape.198), calls=%async_computation.3 | async-start | bytes 16777216 | tf_op jit(solution)/shard_map/all_to_all | solution.py:129
  391.3 99.0 %all-to-all-start.2 = ((bf16[8,2,262144]{2,1,0:T(2,128)(2,1)}), bf16[8,2,262144]{2,1,0:T(2,128)(2,1)}, u32[]{:S(2)}, u32[]{:S(2)}) async-start(bf16[8,2,262144]{2,1,0:T(2,128)(2,1)} %reshape.200), calls=%async_computation.2 | async-start | bytes 16777216 | tf_op jit(solution)/shard_map/all_to_all | solution.py:128
  490.3 154.4 %all-to-all-start.1 = ((bf16[8,1,512,1024]{3,2,1,0:T(8,128)(2,1)}), bf16[8,1,512,1024]{3,2,1,0:T(8,128)(2,1)}, u32[]{:S(2)}, u32[]{:S(2)}) async-start(bf16[8,1,512,1024]{3,2,1,0:T(8,128)(2,1)} %bitcast_dynamic-update-slice_fusion), calls=%async_computation.1 | async-start | bytes 16777216 | tf_op jit(solution)/shard_map/all_to_all | solution.py:123
  495.5 271.5 %reduce-scatter.2.cloned.1.call-start = ((), (), s32[]{:S(2)}) async-start(), calls=%async_computation.8 | async-start | bytes 14155776 | tf_op jit(solution)/shard_map/reduce_scatter | solution.py:40
  604.7 11.0 %copy-start.13 = (bf16[768,2,4096]{2,0,1:T(8,128)(2,1)S(1)}, bf16[768,2,4096]{2,0,1:T(8,128)(2,1)}, u32[]{:S(2)}) copy-start(bf16[768,2,4096]{2,0,1:T(8,128)(2,1)} %all-gather.2.cloned.1.call-done) | copy-start | bytes 37748740
  615.7 22.3 %slice-start = ((s8[8388608]{0:T(1024)(128)(4,1)}), s8[4194304]{0:T(1024)(128)(4,1)S(1)}, s32[]{:S(2)}) async-start(s8[8388608]{0:T(1024)(128)(4,1)} %bitcast.119), calls=%async_computation.9 | async-start | bytes 8388608
  625.9 12.1 %slice-start.1 = ((s8[8388608]{0:T(1024)(128)(4,1)}), s8[4194304]{0:T(1024)(128)(4,1)S(1)}, s32[]{:S(2)}) async-start(s8[8388608]{0:T(1024)(128)(4,1)} %bitcast.119), calls=%async_computation.10 | async-start | bytes 8388608
  644.7 22.3 %slice-start.2 = ((s8[6291456]{0:T(1024)(128)(4,1)}), s8[2097152]{0:T(1024)(128)(4,1)S(1)}, s32[]{:S(2)}) async-start(s8[6291456]{0:T(1024)(128)(4,1)} %bitcast.124), calls=%async_computation.11 | async-start | bytes 4194304
  656.2 10.8 %slice-start.3 = ((s8[6291456]{0:T(1024)(128)(4,1)}), s8[4194304]{0:T(1024)(128)(4,1)S(1)}, s32[]{:S(2)}) async-start(s8[6291456]{0:T(1024)(128)(4,1)} %bitcast.124), calls=%async_computation.12 | async-start | bytes 8388608
  672.5 104.8 %copy-start.14 = (s32[4]{0:T(128)S(1)}, s32[4]{0:T(128)}, u32[]{:S(2)}) copy-start(s32[4]{0:T(128)} %param.30) | copy-start | bytes 52
  672.5 105.0 %copy-start.10 = (f32[128]{0:T(128)S(1)}, f32[128]{0:T(128)}, u32[]{:S(2)}) copy-start(f32[128]{0:T(128)} %copy-done.9) | copy-start | bytes 1540
  672.5 105.0 %copy-start.12 = (f32[128,4]{0,1:T(4,128)S(1)}, f32[128,4]{0,1:T(4,128)}, u32[]{:S(2)}) copy-start(f32[128,4]{0,1:T(4,128)} %get-tuple-element.16) | copy-start | bytes 6148
  672.5 105.1 %copy-start.8 = (f32[128]{0:T(128)S(1)}, f32[128]{0:T(128)}, u32[]{:S(2)}) copy-start(f32[128]{0:T(128)} %copy-done.7) | copy-start | bytes 1540
  672.5 105.1 %copy-start.11 = (f32[128,4]{0,1:T(4,128)S(1)}, f32[128,4]{0,1:T(4,128)}, u32[]{:S(2)}) copy-start(f32[128,4]{0,1:T(4,128)} %get-tuple-element.17) | copy-start | bytes 6148
  672.5 105.1 %copy-start.2 = (s32[128,2]{0,1:T(2,128)S(1)}, s32[128,2]{0,1:T(2,128)}, u32[]{:S(2)}) copy-start(s32[128,2]{0,1:T(2,128)} %param.29) | copy-start | bytes 3076
  672.5 122.1 %copy-start.4 = (s32[256]{0:T(256)S(1)}, s32[256]{0:T(256)}, u32[]{:S(2)}) copy-start(s32[256]{0:T(256)} %copy-done.3) | copy-start | bytes 3076
  672.5 122.1 %copy-start.6 = (s32[256]{0:T(256)S(1)}, s32[256]{0:T(256)}, u32[]{:S(2)}) copy-start(s32[256]{0:T(256)} %copy-done.5) | copy-start | bytes 3076
  772.7 52.6 %all-to-all-start.5 = ((bf16[1,96,2,4096]{1,2,0,3:T(2,128)(2,1)}), bf16[1,96,2,4096]{1,2,0,3:T(2,128)(2,1)S(1)}, u32[]{:S(2)}, u32[]{:S(2)}) async-start(bf16[1,96,2,4096]{1,2,0,3:T(2,128)(2,1)} %copy.107), calls=%async_computation.6 | async-start | bytes 4194304 | tf_op jit(solution)/shard_map/all_to_all | solution.py:44
  831.8 6.3 copy-start.1
Sparse Core Ops, SparseCore 0:
  149.3 141.7 all-gather.1
  672.7 94.2 reduce-scatter.1
